TPU v7x, 32 devices: a whole 2x2x4 slice. The times are simulated.
32 devices in a mesh: section: 4 (over y, core), mp: 8 (over z, x).
Axes of the slice: x: 2, y: 2, z: 4, core: 2. Of those that a mesh axis runs over, the one named last changes fastest.
Arguments:
- arriving: bfloat16 [4, 768, 8192], P('section', None, 'mp'), may hold values from -6 to 6
- norm_gain: bfloat16 [4, 8192], P('section'), may hold values from 0.099609375 to 1.8984375
- w_query: bfloat16 [4, 2048, 8192], P('section', 'mp'), may hold values from -26 to 26
- w_key: bfloat16 [4, 1024, 8192], P('section', 'mp'), may hold values from -1 to 1
- w_value: bfloat16 [4, 1024, 8192], P('section', 'mp'), may hold values from -0.25 to 0.25
- w_out: bfloat16 [4, 2048, 8192], P('section', 'mp'), may hold values from -0.125 to 0.125
Outputs:
- attended: bfloat16 [4, 768, 8192], P('section', 'mp')
- stream_next: bfloat16 [4, 768, 8192], P('section', 'mp')
All inputs are finite; a program needn't handle non-finite values.
Results may differ from a plain program's by a relative error of at most 0.017.
Values may be sent and summed in bfloat16 or wider, within the bound.
A program may use at most 128 MiB of HBM per device.

v0:
```python
import math
import jax
import jax.numpy as jnp
from jax import lax
from jax.sharding import PartitionSpec as P

HD = 128
KV_HEADS = 8
rope_base = 500000.0
norm_eps = 1e-05


def shifted(block, axis, distance):
    devices = range(lax.axis_size(axis))
    route = [((i - distance) % len(devices), i) for i in devices]
    return lax.ppermute(block, axis, route)


def rotate_pairs(channel_major, pair_ids):
    channels = channel_major.shape[0]
    length = channel_major.shape[1]
    frequency = jnp.exp(pair_ids.astype(jnp.float32) * (-2.0 * math.log(rope_base) / HD))
    positions = jnp.arange(length, dtype=jnp.int32).astype(jnp.float32)
    angles = frequency[:, None] * positions[None, :]
    cos_table = jnp.cos(angles)
    sine_table = jnp.sin(angles)
    paired = channel_major.reshape(channels // 2, 2, length)
    even_part = paired[:, 0]
    odd_part = paired[:, 1]
    rotated = jnp.stack(
        [
            even_part * cos_table - odd_part * sine_table,
            even_part * sine_table + odd_part * cos_table,
        ],
        axis=1,
    )
    return rotated.reshape(channels, length)


def head_rows(table, kv_index):
    length = table.shape[1]
    grouped = table.reshape(HD // 2, KV_HEADS, 2, length)
    picked = lax.dynamic_slice_in_dim(grouped, kv_index, 1, 1)
    return picked.reshape(HD, length)


def normalize(hidden_in, gain_row):
    as_float = hidden_in.astype(jnp.float32)
    mean_square = jnp.mean(as_float * as_float, axis=1, keepdims=True)
    normed = (as_float * lax.rsqrt(mean_square + norm_eps) * gain_row).astype(jnp.bfloat16)
    return (as_float, normed)


def channel_product(weights, normed):
    return lax.dot_general(
        weights, normed, (((1,), (1,)), ((), ())), preferred_element_type=jnp.float32
    )


def local(arriving, norm_gain, w_query, w_key, w_value, w_out):
    local_block = arriving[0]
    gain_row = norm_gain[0].astype(jnp.float32)
    query_weights = w_query[0]
    key_weights = w_key[0]
    value_weights = w_value[0]
    out_weights = w_out[0]
    mp_count = lax.axis_size("mp")
    member = lax.axis_index("mp")
    length = local_block.shape[0]
    row_count = length // mp_count
    arrived = shifted(local_block, "section", 1)
    whole_rows = lax.all_gather(arrived, "mp", axis=1, tiled=True)
    full_float, normed_all = normalize(whole_rows, gain_row)
    residual = lax.dynamic_slice_in_dim(full_float, member * row_count, row_count, 0)
    projected = jnp.concatenate(
        [
            channel_product(query_weights, normed_all),
            channel_product(key_weights, normed_all),
            channel_product(value_weights, normed_all),
        ],
        axis=0,
    )
    q_width = query_weights.shape[0]
    k_width = key_weights.shape[0]
    query_pairs = jnp.arange(q_width // 2, dtype=jnp.int32) * 2 % HD // 2
    query_part = rotate_pairs(projected[:q_width], query_pairs).astype(jnp.bfloat16)
    key_pairs = (member * k_width + jnp.arange(k_width // 2, dtype=jnp.int32) * 2) // (2 * KV_HEADS)
    key_part = rotate_pairs(projected[q_width : q_width + k_width], key_pairs).astype(jnp.bfloat16)
    value_part = projected[q_width + k_width :].astype(jnp.bfloat16)
    key_all, value_all = (
        lax.all_gather(key_part, "mp", axis=0, tiled=True),
        lax.all_gather(value_part, "mp", axis=0, tiled=True),
    )
    local_heads = q_width // HD
    group_size = local_heads * mp_count // KV_HEADS
    kv_index = member * local_heads // group_size
    key_head = head_rows(key_all, kv_index)
    value_head = head_rows(value_all, kv_index)
    query_heads = query_part.reshape(local_heads, HD, length)
    score_scale = 1.0 / math.sqrt(HD)
    scores = (
        jnp.einsum("hdi,dj->hij", query_heads, key_head, preferred_element_type=jnp.float32)
        * score_scale
    )
    token_index = jnp.arange(length, dtype=jnp.int32)
    causal = token_index[:, None] >= token_index[None, :]
    scores = jnp.where(causal[None], scores, -1e30)
    row_max = jnp.max(scores, axis=-1, keepdims=True)
    exponent = jnp.exp(scores - row_max)
    row_total = jnp.sum(exponent, axis=-1, keepdims=True)
    weights = (exponent / row_total).astype(jnp.bfloat16)
    context = jnp.einsum(
        "hij,dj->ihd", weights, value_head, preferred_element_type=jnp.float32
    ).astype(jnp.bfloat16)
    context = context.reshape(length, q_width)
    full_term = jnp.dot(context, out_weights, preferred_element_type=jnp.float32)
    summed = lax.psum_scatter(
        full_term.astype(jnp.bfloat16), "mp", scatter_dimension=0, tiled=True
    ).astype(jnp.float32)
    attended = summed.astype(jnp.bfloat16)[None]
    stream_next = (residual + summed).astype(jnp.bfloat16)[None]
    return (attended, stream_next)


def solution(mesh):
    return jax.shard_map(
        local,
        mesh=mesh,
        in_specs=(
            P("section", None, "mp"),
            P("section", None),
            P("section", "mp", None),
            P("section", "mp", None),
            P("section", "mp", None),
            P("section", "mp", None),
        ),
        out_specs=(P("section", "mp", None), P("section", "mp", None)),
        check_vma=False,
    )
```

profile of v0, /device:TPU:0, one launch (start us, length us, event | category | flops | bytes accessed | tf_op | source)
XLA Modules:
  0.0 552.7 jit_solution(1898910907793692140)
XLA Ops:
  7.8 20.4 %collective-permute-done = bf16[768,1024]{1,0:T(8,128)(2,1)} collective-permute-done((bf16[768,1024]{1,0:T(8,128)(2,1)}, bf16[768,1024]{1,0:T(8,128)(2,1)}, u32[]{:S(2)}, u32[]{:S(2)}) %collective-permute-start) | collective-permute-done | bytes 1572896 | tf_op jit(solution)/shard_map/ppermute | solution.py:16
  28.2 0.8 mul.223
  29.0 177.4 %all-gather.4.cloned.1.call-done = bf16[768,8192]{1,0:T(8,128)(2,1)} async-done(((bf16[768,1024]{1,0:T(8,128)(2,1)}), bf16[768,8192]{1,0:T(8,128)(2,1)}) %all-gather.4.cloned.1.call-update) | async-done | bytes 12582928 | tf_op jit(solution)/shard_map/all_gather | solution.py:72
  206.4 7.1 %multiply_reduce_fusion = f32[768]{0:T(1024)S(1)} fusion(bf16[768,8192]{1,0:T(8,128)(2,1)} %all-gather.4.cloned.1.call-done), kind=kLoop, calls=%fused_computation.2 | loop fusion | flops 18873600 | bytes 12585984 | tf_op jit(solution)/shard_map/reduce_sum | solution.py:49
  213.5 7.5 %multiply_convert_fusion = bf16[768,8192]{1,0:T(8,128)(2,1)S(1)} fusion(f32[8192]{0:T(1024)S(1)} %bitcast.56, f32[768]{0:T(1024)S(1)} %add_rsqrt_fusion, bf16[768,8192]{1,0:T(8,128)(2,1)} %all-gather.4.cloned.1.call-done), kind=kLoop, calls=%fused_computation.1 | loop fusion | flops 25165824 | bytes 25201664 | tf_op jit(solution)/shard_map/convert_element_type | solution.py:50
  221.0 4.5 copy-done.2
  225.5 4.1 fusion.24
  229.7 9.4 %fusion.18 = f32[128,768]{1,0:T(8,128)S(1)} fusion(bf16[768,8192]{1,0:T(8,128)(2,1)} %copy-done.2, bf16[1,128,8192]{2,1,0:T(8,128)(2,1)} %param.9), kind=kOutput, calls=%fused_computation.24 | convolution fusion | flops 1610612736 | bytes 15073280 | tf_op jit(solution)/shard_map/dot_general | solution.py:55
  239.8 0.8 fusion.42
  240.8 0.8 convert_element_type.92
  241.9 14.1 %fusion.14 = f32[256,768]{1,0:T(8,128)S(1)} fusion(bf16[768,8192]{1,0:T(8,128)(2,1)} %copy-done.2, bf16[1,256,8192]{2,1,0:T(8,128)(2,1)} %param.8), kind=kOutput, calls=%fused_computation.22 | convolution fusion | flops 3221225472 | bytes 17563648 | tf_op jit(solution)/shard_map/dot_general | solution.py:55
  257.0 1.7 fusion.34
  259.3 13.1 %all-gather.6.cloned.1.call-done = bf16[1024,768]{0,1:T(8,128)(2,1)} async-done(((bf16[128,768]{0,1:T(8,128)(2,1)}), bf16[1024,768]{0,1:T(8,128)(2,1)}) %all-gather.6.cloned.1.call-update) | async-done | bytes 1572880 | tf_op jit(solution)/shard_map/all_gather | solution.py:92
  272.4 1.7 copy.16
  274.1 1.5 reshape.281
  275.6 42.1 %all-gather.8.cloned.1.call-done = bf16[1024,768]{1,0:T(8,128)(2,1)} async-done(((bf16[128,768]{1,0:T(8,128)(2,1)}), bf16[1024,768]{1,0:T(8,128)(2,1)}) %all-gather.8.cloned.1.call-update) | async-done | bytes 1572880 | tf_op jit(solution)/shard_map/all_gather | solution.py:91
  317.7 3.5 reshape.285
  321.2 1.2 constant_dynamic-slice_fusion
  322.6 3.8 fusion.57
  326.4 3.0 fusion.17
  330.0 6.3 %convolution_convert_fusion = bf16[768,8192]{1,0:T(8,128)(2,1)} fusion(bf16[768,256]{0,1:T(8,128)(2,1)S(1)} %bitcast.55, bf16[1,256,8192]{2,1,0:T(8,128)(2,1)S(1)} %copy-done.3), kind=kOutput, calls=%fused_computation.3 | convolution fusion | flops 3227516928 | bytes 17170432 | tf_op jit(solution)/shard_map/dot_general | solution.py:116
  336.4 14.5 %convert_element_type.84 = f32[768,8192]{1,0:T(8,128)} convert(bf16[768,8192]{1,0:T(8,128)(2,1)} %all-gather.4.cloned.1.call-done) | non-fusion elementwise | flops 6291456 | bytes 37748736 | tf_op jit(solution)/shard_map/convert_element_type | solution.py:48
  350.9 191.5 %reduce-scatter.2.cloned.1.call-done = bf16[96,8192]{1,0:T(8,128)(2,1)} async-done(((bf16[768,8192]{1,0:T(8,128)(2,1)}), bf16[96,8192]{1,0:T(8,128)(2,1)}) %reduce-scatter.2.cloned.1.call-update) | async-done | bytes 1572880 | tf_op jit(solution)/shard_map/reduce_scatter | solution.py:117
  542.4 3.8 fusion.13
  (32 shorter events, 4.2 us)
Async XLA Ops:
  7.2 218.4 %copy-start = (bf16[1,128,8192]{2,1,0:T(8,128)(2,1)S(1)}, bf16[1,128,8192]{2,1,0:T(8,128)(2,1)}, u32[]{:S(2)}) copy-start(bf16[1,128,8192]{2,1,0:T(8,128)(2,1)} %param.10) | copy-start | bytes 6291460
  7.2 199.3 %all-gather.4.cloned.1.call-start = ((), (), s32[]{:S(2)}) async-start(), calls=%async_computation.1 | async-start | bytes 14155776 | tf_op jit(solution)/shard_map/all_gather | solution.py:72
  7.2 20.9 %collective-permute-start = (bf16[768,1024]{1,0:T(8,128)(2,1)}, bf16[768,1024]{1,0:T(8,128)(2,1)}, u32[]{:S(2)}, u32[]{:S(2)}) collective-permute-start(bf16[768,1024]{1,0:T(8,128)(2,1)} %bitcast.57), channel_id=1, source_target_pairs={{24,0},{0,8},{8,16},{16,24},{25,1},{1,9},{9,17},{17,25},{26,2},{2,... | collective-permute-start | bytes 4718600 | tf_op jit(solution)/shard_map/ppermute | solution.py:16
  28.2 244.3 %all-gather.6.cloned.1.call-start = ((), (), s32[]{:S(2)}) async-start(), calls=%async_computation.2 | async-start | bytes 1769472 | tf_op jit(solution)/shard_map/all_gather | solution.py:92
  221.0 4.5 copy-start.2
  229.7 88.0 %all-gather.8.cloned.1.call-start = ((), (), s32[]{:S(2)}) async-start(), calls=%async_computation.3 | async-start | bytes 1769472 | tf_op jit(solution)/shard_map/all_gather | solution.py:91
  241.6 300.8 %reduce-scatter.2.cloned.1.call-start = ((), (), s32[]{:S(2)}) async-start(), calls=%async_computation.4 | async-start | bytes 14155776 | tf_op jit(solution)/shard_map/reduce_scatter | solution.py:117
  326.4 3.6 copy-start.3
  336.4 209.8 %copy-start.1 = (bf16[1,128,8192]{2,1,0:T(8,128)(2,1)S(1)}, bf16[1,128,8192]{2,1,0:T(8,128)(2,1)}, u32[]{:S(2)}) copy-start(bf16[1,128,8192]{2,1,0:T(8,128)(2,1)} %param.10) | copy-start | bytes 6291460
Sparse Core Ops, SparseCore 0:
  28.3 178.1 all-gather.3
  229.8 42.5 all-gather.5
  275.2 42.4 all-gather.7
  336.5 205.7 reduce-scatter.1
where the time goes:
time: 553 us
  waiting for transfers between devices  445 us (80%)
  matrix products  40.7 us (7%)
  other arithmetic  36.4 us (7%)
  local copies, waits for them, and re-layouts  16.4 us (3%)
  between operations  14 us (3%)
    reduce_scatter x1, waiting for transfers between devices, local(): lax.psum_scatter(full_term.astype(jnp.bfloat16), 'mp', scatter_dimension=...  191 us
    all_gather x1, waiting for transfers between devices, local(): whole_rows = lax.all_gather(arrived, 'mp', axis=1, tiled=True)  177 us
    all_gather x1, waiting for transfers between devices, local(): lax.all_gather(key_part, 'mp', axis=0, tiled=True)  42.1 us
    dot_general x3, matrix products, channel_product(): lax.dot_general(weights, normed, (((1,), (1,)), ((), ())), preferred_elem...  27.6 us
    ppermute x1, waiting for transfers between devices, shifted(): return lax.ppermute(block, axis, route)  20.4 us
    convert_element_type x1, other arithmetic, normalize(): as_float = hidden_in.astype(jnp.float32)  14.5 us
    all_gather x1, waiting for transfers between devices, local(): lax.all_gather(value_part, 'mp', axis=0, tiled=True)  13.1 us
  transfers between devices with their start and end apart: 5, of which 5 were waited for; matrix products, arithmetic and copies ran while one was open for 9% of the time, Pallas kernels for 0%

commit v1 on v0

--- a/solution.py
+++ b/solution.py
@@ -8,6 +8,12 @@
 KV_HEADS = 8
 rope_base = 500000.0
 norm_eps = 1e-05
+
+
+def gathered_along(x, name, dim):
+    parts = lax.all_gather(x, name, axis=0, tiled=False)
+    whole = jnp.concatenate(parts, axis=dim)
+    return whole
 
 
 def shifted(block, axis, distance):
@@ -69,7 +75,7 @@
     length = local_block.shape[0]
     row_count = length // mp_count
     arrived = shifted(local_block, "section", 1)
-    whole_rows = lax.all_gather(arrived, "mp", axis=1, tiled=True)
+    whole_rows = gathered_along(arrived, "mp", 1)
     full_float, normed_all = normalize(whole_rows, gain_row)
     residual = lax.dynamic_slice_in_dim(full_float, member * row_count, row_count, 0)
     projected = jnp.concatenate(

time: 553 us -> 573 us (1.036)
  local copies, waits for them, and re-layouts: 16.4 us -> 36.8 us
    convert_element_type x2 -> x0, other arithmetic: 21.9 us -> none  [the longest x1 14.5 us: normalize(): as_float = hidden_in.astype(jnp.float32)]
    mul x0 -> x2, local copies, waits for them, and re-layouts: none -> 16.3 us  [normalize(): as_float * lax.rsqrt(mean_square + norm_eps) * gain_row]
    mul x1 -> x2, other arithmetic: 0.79 us -> 13 us  [normalize(): as_float * lax.rsqrt(mean_square + norm_eps) * gain_row]
    convert_element_type x0 -> x1, local copies, waits for them, and re-layouts: none -> 8.65 us  [normalize(): as_float = hidden_in.astype(jnp.float32)]
    unnamed x0 -> x1, other arithmetic: none -> 7.76 us
    all_gather x1, waiting for transfers between devices: 13.1 us -> 20.7 us  [local(): lax.all_gather(value_part, 'mp', axis=0, tiled=True)]
  transfers between devices with their start and end apart: 5 -> 5, of which waited for: 5 -> 5; matrix products, arithmetic and copies ran while one was open for 9% -> 7% of each run, Pallas kernels for 0% -> 0%
where the time goes in v1:
time: 573 us; the launch traced here: 572 us
  waiting for transfers between devices  450 us (79%)
  local copies, waits for them, and re-layouts  36.8 us (6%)
  matrix products  36.3 us (6%)
  other arithmetic  34.4 us (6%)
  between operations  14 us (2%)
    reduce_scatter x1, waiting for transfers between devices, local(): lax.psum_scatter(full_term.astype(jnp.bfloat16), 'mp', scatter_dimension=...  190 us
    all_gather x1, waiting for transfers between devices, gathered_along(): parts = lax.all_gather(x, name, axis=0, tiled=False)  177 us
    all_gather x1, waiting for transfers between devices, local(): lax.all_gather(key_part, 'mp', axis=0, tiled=True)  41.9 us
    dot_general x3, matrix products, channel_product(): lax.dot_general(weights, normed, (((1,), (1,)), ((), ())), preferred_elem...  23.2 us
    all_gather x1, waiting for transfers between devices, local(): lax.all_gather(value_part, 'mp', axis=0, tiled=True)  20.7 us
    ppermute x1, waiting for transfers between devices, shifted(): return lax.ppermute(block, axis, route)  20.4 us
    mul x2, local copies, waits for them, and re-layouts, normalize(): as_float * lax.rsqrt(mean_square + norm_eps) * gain_row  16.3 us
    mul x2, other arithmetic, normalize(): as_float * lax.rsqrt(mean_square + norm_eps) * gain_row  13 us
  transfers between devices with their start and end apart: 5, of which 5 were waited for; matrix products, arithmetic and copies ran while one was open for 7% of the time, Pallas kernels for 0%

profile of v1, /device:TPU:0, one launch (start us, length us, event | category | flops | bytes accessed | tf_op | source)
XLA Modules:
  0.0 572.1 jit_solution(11664445280410154016)
XLA Ops:
  7.8 20.4 %collective-permute-done = bf16[768,1024]{1,0:T(8,128)(2,1)} collective-permute-done((bf16[768,1024]{1,0:T(8,128)(2,1)}, bf16[768,1024]{1,0:T(8,128)(2,1)}, u32[]{:S(2)}, u32[]{:S(2)}) %collective-permute-start) | collective-permute-done | bytes 1572896 | tf_op jit(solution)/shard_map/ppermute | solution.py:22
  28.2 0.8 convert_reduce_fusion
  29.1 177.4 %all-gather.9.cloned.1.call-done = bf16[6144,1024]{1,0:T(8,128)(2,1)} async-done(((bf16[768,1024]{1,0:T(8,128)(2,1)}), bf16[6144,1024]{1,0:T(8,128)(2,1)}) %all-gather.9.cloned.1.call-update) | async-done | bytes 12582928 | tf_op jit(solution)/shard_map/all_gather | solution.py:14
  206.4 7.1 %fusion.1 = f32[768]{0:T(1024)S(1)} fusion(bf16[8,768,1024]{2,1,0:T(8,128)(2,1)} %bitcast.62), kind=kLoop, calls=%fused_computation.4 | loop fusion | flops 18873600 | bytes 12585984 | tf_op jit(solution)/shard_map/reduce_sum | solution.py:55
  213.5 12.2 %fusion.4 = bf16[768,8,1024]{2,0,1:T(8,128)(2,1)} fusion(bf16[8,768,1024]{2,1,0:T(8,128)(2,1)} %bitcast.63, f32[8,1024]{1,0:T(8,128)S(1)} %reshape.326, f32[768]{0:T(1024)S(1)} %add_rsqrt_fusion), kind=kLoop, calls=%fused_computation.8 | loop fusion | flops 25165824 | bytes 25201664 | tf_op jit(solution)/shard_map/mul | solution.py:56
  225.7 16.3 %copy.25 = bf16[768,8,1024]{0,2,1:T(8,128)(2,1)} copy(bf16[768,8,1024]{2,0,1:T(8,128)(2,1)} %fusion.4) | data formatting | bytes 25165824 | tf_op jit(solution)/shard_map/mul | solution.py:56
  242.0 7.1 %fusion.28 = bf16[128,768]{0,1:T(8,128)(2,1)} fusion(bf16[768,8192]{0,1:T(8,128)(2,1)} %bitcast.65, bf16[1,128,8192]{2,1,0:T(8,128)(2,1)S(1)} %copy-done), kind=kOutput, calls=%fused_computation.31 | convolution fusion | flops 1610711040 | bytes 14876672 | tf_op jit(solution)/shard_map/dot_general | solution.py:61
  249.2 7.0 %fusion.22 = f32[128,768]{1,0:T(8,128)S(1)} fusion(bf16[768,8192]{0,1:T(8,128)(2,1)} %bitcast.66, bf16[1,128,8192]{2,1,0:T(8,128)(2,1)} %param.9), kind=kOutput, calls=%fused_computation.29 | convolution fusion | flops 1610612736 | bytes 15073280 | tf_op jit(solution)/shard_map/dot_general | solution.py:61
  256.8 0.8 fusion.46
  258.9 9.1 %fusion.18 = f32[256,768]{1,0:T(8,128)S(1)} fusion(bf16[768,8192]{0,1:T(8,128)(2,1)} %bitcast.67, bf16[1,256,8192]{2,1,0:T(8,128)(2,1)} %param.8), kind=kOutput, calls=%fused_computation.27 | convolution fusion | flops 3221225472 | bytes 17563648 | tf_op jit(solution)/shard_map/dot_general | solution.py:61
  269.0 1.7 fusion.38
  271.3 20.7 %all-gather.5.cloned.1.call-done = bf16[1024,768]{0,1:T(8,128)(2,1)} async-done(((bf16[128,768]{0,1:T(8,128)(2,1)}), bf16[1024,768]{0,1:T(8,128)(2,1)}) %all-gather.5.cloned.1.call-update) | async-done | bytes 1572880 | tf_op jit(solution)/shard_map/all_gather | solution.py:98
  292.0 1.7 copy.26
  293.7 1.5 reshape.319
  295.2 41.9 %all-gather.7.cloned.1.call-done = bf16[1024,768]{1,0:T(8,128)(2,1)} async-done(((bf16[128,768]{1,0:T(8,128)(2,1)}), bf16[1024,768]{1,0:T(8,128)(2,1)}) %all-gather.7.cloned.1.call-update) | async-done | bytes 1572880 | tf_op jit(solution)/shard_map/all_gather | solution.py:97
  337.1 3.5 reshape.323
  340.7 1.2 constant_dynamic-slice_fusion
  342.1 3.8 fusion.61
  345.8 3.0 fusion.21
  349.4 6.4 %convolution_convert_fusion = bf16[768,8192]{1,0:T(8,128)(2,1)} fusion(bf16[768,256]{0,1:T(8,128)(2,1)S(1)} %bitcast.70, bf16[1,256,8192]{2,1,0:T(8,128)(2,1)S(1)} %copy-done.2), kind=kOutput, calls=%fused_computation.7 | convolution fusion | flops 3227516928 | bytes 17170432 | tf_op jit(solution)/shard_map/dot_general | solution.py:122
  355.8 7.8 %convert_bitcast_fusion = f32[8,96,8,1024]{3,2,1,0:T(8,128)S(1)} fusion(bf16[8,768,1024]{2,1,0:T(8,128)(2,1)} %bitcast.64), kind=kLoop, calls=%fused_computation.1 | loop fusion | flops 6291456 | bytes 37748736
  363.6 8.6 %copy.43 = f32[8,96,8,1024]{3,2,0,1:T(8,128)} copy(f32[8,96,8,1024]{3,2,1,0:T(8,128)S(1)} %convert_bitcast_fusion) | data formatting | bytes 50331648 | tf_op jit(solution)/shard_map/convert_element_type | solution.py:54
  372.2 189.5 %reduce-scatter.2.cloned.1.call-done = bf16[96,8192]{1,0:T(8,128)(2,1)} async-done(((bf16[768,8192]{1,0:T(8,128)(2,1)}), bf16[96,8192]{1,0:T(8,128)(2,1)}) %reduce-scatter.2.cloned.1.call-update) | async-done | bytes 1572880 | tf_op jit(solution)/shard_map/reduce_scatter | solution.py:123
  561.8 3.8 fusion.17
  (33 shorter events, 5.0 us)
Async XLA Ops:
  7.2 234.8 %copy-start = (bf16[1,128,8192]{2,1,0:T(8,128)(2,1)S(1)}, bf16[1,128,8192]{2,1,0:T(8,128)(2,1)}, u32[]{:S(2)}) copy-start(bf16[1,128,8192]{2,1,0:T(8,128)(2,1)} %param.10) | copy-start | bytes 6291460
  7.2 199.3 %all-gather.9.cloned.1.call-start = ((), (), s32[]{:S(2)}) async-start(), calls=%async_computation.4 | async-start | bytes 14155776 | tf_op jit(solution)/shard_map/all_gather | solution.py:14
  7.2 20.9 %collective-permute-start = (bf16[768,1024]{1,0:T(8,128)(2,1)}, bf16[768,1024]{1,0:T(8,128)(2,1)}, u32[]{:S(2)}, u32[]{:S(2)}) collective-permute-start(bf16[768,1024]{1,0:T(8,128)(2,1)} %bitcast.71), channel_id=1, source_target_pairs={{24,0},{0,8},{8,16},{16,24},{25,1},{1,9},{9,17},{17,25},{26,2},{2,... | collective-permute-start | bytes 4718600 | tf_op jit(solution)/shard_map/ppermute | solution.py:22
  28.2 263.8 %all-gather.5.cloned.1.call-start = ((), (), s32[]{:S(2)}) async-start(), calls=%async_computation.1 | async-start | bytes 1769472 | tf_op jit(solution)/shard_map/all_gather | solution.py:98
  249.1 88.0 %all-gather.7.cloned.1.call-start = ((), (), s32[]{:S(2)}) async-start(), calls=%async_computation.2 | async-start | bytes 1769472 | tf_op jit(solution)/shard_map/all_gather | solution.py:97
  258.6 303.2 %reduce-scatter.2.cloned.1.call-start = ((), (), s32[]{:S(2)}) async-start(), calls=%async_computation.3 | async-start | bytes 14155776 | tf_op jit(solution)/shard_map/reduce_scatter | solution.py:123
  345.8 3.6 copy-start.2
  363.6 202.0 %copy-start.1 = (bf16[1,128,8192]{2,1,0:T(8,128)(2,1)S(1)}, bf16[1,128,8192]{2,1,0:T(8,128)(2,1)}, u32[]{:S(2)}) copy-start(bf16[1,128,8192]{2,1,0:T(8,128)(2,1)} %param.10) | copy-start | bytes 6291460
Sparse Core Ops, SparseCore 0:
  28.3 178.1 all-gather.8
  249.2 42.6 all-gather.4
  294.7 42.3 all-gather.6
  355.9 205.7 reduce-scatter.1
